TPU v7x, 32 devices: a whole 2x2x4 slice. The times are simulated.
32 devices in a mesh: rows: 16 (over z, y, core), cols: 2 (over x).
Axes of the slice: x: 2, y: 2, z: 4, core: 2. Of those that a mesh axis runs over, the one named last changes fastest.
Arguments:
- initial_field: float32 [16384, 4096], P(('rows', 'cols')), may hold values from -6 to 6
- diffusion: bfloat16 [16384, 4096], P(('rows', 'cols')), may hold values from 16 to 8192
Outputs:
- final_field: float32 [16384, 4096], P(('rows', 'cols'))
All inputs are finite; a program needn't handle non-finite values.
Results may differ from a plain program's by a relative error of at most 0.0004.
Values may be sent and summed in bfloat16 or wider, within the bound.
A program may use at most 320 MiB of HBM per device.

v0:
```python
import jax
import jax.numpy as jnp
from jax import lax
from jax.sharding import PartitionSpec as P

ITERS = 2


def lift_lines(values):
    return jnp.concatenate([values[1:], jnp.zeros_like(values[:1])], axis=0)


def lower_lines(values):
    return jnp.concatenate([jnp.zeros_like(values[:1]), values[:-1]], axis=0)


def reduce_solve(lower_band, upper_band, right_side):
    length = right_side.shape[0]
    batch = right_side.shape[1]
    if length == 1:
        return right_side
    halved = length // 2
    lower_pair = lower_band.reshape(halved, 2, batch)
    upper_pair = upper_band.reshape(halved, 2, batch)
    right_pair = right_side.reshape(halved, 2, batch)
    lower_even = lower_pair[:, 0]
    lower_odd = lower_pair[:, 1]
    upper_even = upper_pair[:, 0]
    upper_odd = upper_pair[:, 1]
    right_even = right_pair[:, 0]
    right_odd = right_pair[:, 1]
    divisor = 1.0 - lower_odd * upper_even - upper_odd * lift_lines(lower_even)
    coarse = reduce_solve(
        lower_odd * lower_even / divisor,
        upper_odd * lift_lines(upper_even) / divisor,
        (right_odd + lower_odd * right_even + upper_odd * lift_lines(right_even)) / divisor,
    )
    even_values = right_even + lower_even * lower_lines(coarse) + upper_even * coarse
    return jnp.stack([even_values, coarse], axis=1).reshape(length, batch)


def solve_lines(coefficient, right_side):
    scaled = 1.0 + 2.0 * coefficient
    ratios = coefficient / scaled
    return reduce_solve(ratios, ratios, right_side / scaled)


def add_line_term(current, coefficient):
    return current + coefficient * (lower_lines(current) - 2.0 * current + lift_lines(current))


def toward_x_lines(across_first):
    return lax.all_to_all(across_first, ("rows", "cols"), split_axis=1, concat_axis=0, tiled=True)


def toward_y_lines(along_x):
    return lax.all_to_all(along_x, ("rows", "cols"), split_axis=0, concat_axis=1, tiled=True).T


def local(initial_field, diffusion):
    coupling_y = 0.5 * diffusion.T.astype(jnp.float32)
    turned_numbers = lax.all_to_all(
        diffusion, ("rows", "cols"), split_axis=1, concat_axis=0, tiled=True
    )
    coupling_x = 0.5 * turned_numbers.astype(jnp.float32)
    state_y = initial_field.T
    for iteration in range(ITERS):
        right_side = toward_x_lines(add_line_term(state_y, coupling_y).T)
        middle = solve_lines(coupling_x, right_side)
        right_back = toward_y_lines(add_line_term(middle, coupling_x))
        state_y = solve_lines(coupling_y, right_back)
    return state_y.T


def solution(mesh):
    in_specs = (P(("rows", "cols"), None), P(("rows", "cols"), None))
    out_specs = P(("rows", "cols"), None)
    return jax.shard_map(local, mesh=mesh, in_specs=in_specs, out_specs=out_specs, check_vma=False)
```

profile of v0, /device:TPU:0, one launch (start us, length us, event | category | flops | bytes accessed | tf_op | source)
XLA Modules:
  0.0 1860.7 jit_solution(13646214231910423299)
XLA Ops:
  23.0 12.6 fusion.123
  47.6 60.1 %all-to-all-done.1 = bf16[512,32,128]{0,2,1:T(8,128)(2,1)} async-done(((bf16[512,32,128]{0,2,1:T(8,128)(2,1)}), bf16[512,32,128]{0,2,1:T(8,128)(2,1)}, u32[]{:S(2)}, u32[]{:S(2)}) %all-to-all-start.1) | async-done | bytes 4194336 | tf_op jit(solution)/shard_map/all_to_all | solution.py:62
  107.6 188.5 %all_to_all.77 = f32[512,32,128]{0,2,1:T(8,128)S(1)} all-to-all(f32[512,32,128]{0,2,1:T(8,128)} %bitcast.1742), channel_id=1, replica_groups=mesh['rows'=16,'cols'=2] {'rows','cols'}, dimensions={1} | all-to-all | bytes 16777216 | tf_op jit(solution)/shard_map/all_to_all | solution.py:53
  296.2 11.6 fusion.3
  395.0 14.8 fusion.129
  469.0 15.6 copy.3807
  493.6 14.4 copy.3809
  514.7 13.5 fusion.16
  528.3 187.3 %all_to_all.78 = f32[32,512,128]{2,1,0:T(8,128)} all-to-all(f32[32,512,128]{2,1,0:T(8,128)} %bitcast.1732), channel_id=1, replica_groups=mesh['rows'=16,'cols'=2] {'rows','cols'}, dimensions={0} | all-to-all | bytes 16777216 | tf_op jit(solution)/shard_map/all_to_all | solution.py:57
  734.4 10.5 reshape.819
  751.9 11.5 fusion.118
  763.4 10.5 reshape.818
  779.3 10.9 fusion.119
  1122.8 16.5 copy.3914
  1139.3 10.9 reshape.864
  1150.2 12.6 fusion.117
  1174.9 187.6 %all_to_all.79 = f32[512,32,128]{0,2,1:T(8,128)S(1)} all-to-all(f32[512,32,128]{0,2,1:T(8,128)} %bitcast.1743), channel_id=1, replica_groups=mesh['rows'=16,'cols'=2] {'rows','cols'}, dimensions={1} | all-to-all | bytes 16777216 | tf_op jit(solution)/shard_map/all_to_all | solution.py:53
  1428.9 15.9 copy.3976
  1453.7 14.4 copy.3978
  1474.6 13.5 fusion.17
  1488.1 187.5 %all_to_all.80 = f32[32,512,128]{2,1,0:T(8,128)} all-to-all(f32[32,512,128]{2,1,0:T(8,128)} %bitcast.1731), channel_id=1, replica_groups=mesh['rows'=16,'cols'=2] {'rows','cols'}, dimensions={0} | all-to-all | bytes 16777216 | tf_op jit(solution)/shard_map/all_to_all | solution.py:57
  1693.9 10.5 reshape.892
  1824.2 16.5 copy.4032
  1840.7 10.9 reshape.915
  (1127 shorter events, 795.8 us)
Async XLA Ops:
  6.5 101.1 %all-to-all-start.1 = ((bf16[512,32,128]{0,2,1:T(8,128)(2,1)}), bf16[512,32,128]{0,2,1:T(8,128)(2,1)}, u32[]{:S(2)}, u32[]{:S(2)}) async-start(bf16[512,32,128]{0,2,1:T(8,128)(2,1)} %bitcast.1697), calls=%async_computation.1 | async-start | bytes 8388608 | tf_op jit(solution)/shard_map/all_to_all | solution.py:62
  393.5 74.6 %copy-start.33 = (f32[4096,1,128]{2,1,0:T(1,128)}, f32[4096,1,128]{2,1,0:T(1,128)S(1)}, u32[]{:S(2)}) copy-start(f32[4096,1,128]{2,1,0:T(1,128)S(1)} %get-tuple-element.97) | copy-start | bytes 6291460
  421.9 38.0 %copy-start.63 = (f32[2048,1,128]{2,1,0:T(1,128)}, f32[2048,1,128]{2,1,0:T(1,128)S(1)}, u32[]{:S(2)}) copy-start(f32[2048,1,128]{2,1,0:T(1,128)S(1)} %get-tuple-element.115) | copy-start | bytes 3145732
  431.0 26.3 %copy-start.126 = (f32[512,1,128]{2,1,0:T(1,128)}, f32[512,1,128]{2,1,0:T(1,128)S(1)}, u32[]{:S(2)}) copy-start(f32[512,1,128]{2,1,0:T(1,128)S(1)} %get-tuple-element.155) | copy-start | bytes 786436
  826.4 57.3 %copy-start.28 = (f32[1024,1,512]{2,1,0:T(1,128)}, f32[1024,1,512]{2,1,0:T(1,128)S(1)}, u32[]{:S(2)}) copy-start(f32[1024,1,512]{2,1,0:T(1,128)S(1)} %get-tuple-element.87) | copy-start | bytes 6291460
  896.7 180.7 %copy-start.68 = (f32[512,1,512]{2,1,0:T(1,128)}, f32[512,1,512]{2,1,0:T(1,128)S(1)}, u32[]{:S(2)}) copy-start(f32[512,1,512]{2,1,0:T(1,128)S(1)} %get-tuple-element.107) | copy-start | bytes 3145732
  929.8 140.5 %copy-start.100 = (f32[256,1,512]{2,1,0:T(1,128)}, f32[256,1,512]{2,1,0:T(1,128)S(1)}, u32[]{:S(2)}) copy-start(f32[256,1,512]{2,1,0:T(1,128)S(1)} %get-tuple-element.127) | copy-start | bytes 1572868
  937.0 133.2 %copy-start.102 = (f32[256,1,512]{2,1,0:T(1,128)}, f32[256,1,512]{2,1,0:T(1,128)S(1)}, u32[]{:S(2)}) copy-start(f32[256,1,512]{2,1,0:T(1,128)S(1)} %get-tuple-element.125) | copy-start | bytes 1572868
  954.2 111.1 %copy-start.130 = (f32[128,1,512]{2,1,0:T(1,128)}, f32[128,1,512]{2,1,0:T(1,128)S(1)}, u32[]{:S(2)}) copy-start(f32[128,1,512]{2,1,0:T(1,128)S(1)} %get-tuple-element.147) | copy-start | bytes 786436
  971.8 89.4 %copy-start.154 = (f32[64,1,512]{2,1,0:T(1,128)}, f32[64,1,512]{2,1,0:T(1,128)S(1)}, u32[]{:S(2)}) copy-start(f32[64,1,512]{2,1,0:T(1,128)S(1)} %get-tuple-element.167) | copy-start | bytes 393220
  973.3 87.9 %copy-start.156 = (f32[64,1,512]{2,1,0:T(1,128)}, f32[64,1,512]{2,1,0:T(1,128)S(1)}, u32[]{:S(2)}) copy-start(f32[64,1,512]{2,1,0:T(1,128)S(1)} %get-tuple-element.165) | copy-start | bytes 393220
  976.1 80.2 %copy-start.161 = (f32[64,512]{1,0:T(8,128)}, f32[64,512]{1,0:T(8,128)S(1)}, u32[]{:S(2)}) copy-start(f32[64,512]{1,0:T(8,128)S(1)} %get-tuple-element.20) | copy-start | bytes 393220
  978.5 80.1 %copy-start.185 = (f32[32,1,512]{2,1,0:T(1,128)S(1)}, f32[32,1,512]{2,1,0:T(1,128)}, u32[]{:S(2)}) copy-start(f32[32,1,512]{2,1,0:T(1,128)} %get-tuple-element.191) | copy-start | bytes 196612
  982.0 79.2 %copy-start.168 = (f32[32,1,512]{2,1,0:T(1,128)}, f32[32,1,512]{2,1,0:T(1,128)S(1)}, u32[]{:S(2)}) copy-start(f32[32,1,512]{2,1,0:T(1,128)S(1)} %get-tuple-element.188) | copy-start | bytes 196612
  982.0 79.2 %copy-start.176 = (f32[32,1,512]{2,1,0:T(1,128)}, f32[32,1,512]{2,1,0:T(1,128)S(1)}, u32[]{:S(2)}) copy-start(f32[32,1,512]{2,1,0:T(1,128)S(1)} %get-tuple-element.187) | copy-start | bytes 196612
  983.2 78.0 %copy-start.170 = (f32[32,1,512]{2,1,0:T(1,128)}, f32[32,1,512]{2,1,0:T(1,128)S(1)}, u32[]{:S(2)}) copy-start(f32[32,1,512]{2,1,0:T(1,128)S(1)} %get-tuple-element.186) | copy-start | bytes 196612
  983.2 78.0 %copy-start.178 = (f32[32,1,512]{2,1,0:T(1,128)}, f32[32,1,512]{2,1,0:T(1,128)S(1)}, u32[]{:S(2)}) copy-start(f32[32,1,512]{2,1,0:T(1,128)S(1)} %get-tuple-element.185) | copy-start | bytes 196612
  985.7 75.5 %copy-start.183 = (f32[32,512]{1,0:T(8,128)}, f32[32,512]{1,0:T(8,128)S(1)}, u32[]{:S(2)}) copy-start(f32[32,512]{1,0:T(8,128)S(1)} %get-tuple-element.18) | copy-start | bytes 196612
  990.7 74.6 %copy-start.133 = (f32[128,1,512]{2,1,0:T(1,128)S(1)}, f32[128,1,512]{2,1,0:T(1,128)}, u32[]{:S(2)}) copy-start(f32[128,1,512]{2,1,0:T(1,128)} %copy-done.132) | copy-start | bytes 786436
  991.6 67.0 %copy-start.196 = (f32[16,1,512]{2,1,0:T(1,128)}, f32[16,1,512]{2,1,0:T(1,128)S(1)}, u32[]{:S(2)}) copy-start(f32[16,1,512]{2,1,0:T(1,128)S(1)} %get-tuple-element.207) | copy-start | bytes 98308
  991.7 69.5 %copy-start.190 = (f32[16,1,512]{2,1,0:T(1,128)}, f32[16,1,512]{2,1,0:T(1,128)S(1)}, u32[]{:S(2)}) copy-start(f32[16,1,512]{2,1,0:T(1,128)S(1)} %get-tuple-element.208) | copy-start | bytes 98308
  995.0 63.7 %copy-start.198 = (f32[16,1,512]{2,1,0:T(1,128)}, f32[16,1,512]{2,1,0:T(1,128)S(1)}, u32[]{:S(2)}) copy-start(f32[16,1,512]{2,1,0:T(1,128)S(1)} %get-tuple-element.205) | copy-start | bytes 98308
  995.0 66.2 %copy-start.191 = (f32[16,1,512]{2,1,0:T(1,128)}, f32[16,1,512]{2,1,0:T(1,128)S(1)}, u32[]{:S(2)}) copy-start(f32[16,1,512]{2,1,0:T(1,128)S(1)} %get-tuple-element.206) | copy-start | bytes 98308
  1007.8 58.8 %copy-start.208 = (f32[8,1,512]{2,1,0:T(1,128)}, f32[8,1,512]{2,1,0:T(1,128)S(1)}, u32[]{:S(2)}) copy-start(f32[8,1,512]{2,1,0:T(1,128)S(1)} %get-tuple-element.228) | copy-start | bytes 49156
  (249 other events, 1180.7 us)
where the time goes:
time: 1870 us; the launch traced here: 1860 us
  local copies, waits for them, and re-layouts  794 us (42%)
  blocking collectives  751 us (40%)
  other arithmetic  242 us (13%)
  waiting for transfers between devices  60.1 us (3%)
    all_to_all x2, blocking collectives, toward_x_lines(): lax.all_to_all(across_first, ('rows', 'cols'), split_axis=1, concat_axis=...  376 us
    all_to_all x2, blocking collectives, toward_y_lines(): lax.all_to_all(along_x, ('rows', 'cols'), split_axis=0, concat_axis=1, ti...  375 us
    another operation x68, local copies, waits for them, and re-layouts, reduce_solve(): return jnp.stack([even_values, coarse], axis=1).reshape(length, batch)  165 us
    slice x95, local copies, waits for them, and re-layouts, lift_lines(): return jnp.concatenate([values[1:], jnp.zeros_like(values[:1])], axis=0)  117 us
    slice x48, local copies, waits for them, and re-layouts, reduce_solve(): right_even = right_pair[:, 0]  87.7 us
    another operation x100, other arithmetic, reduce_solve(): return jnp.stack([even_values, coarse], axis=1).reshape(length, batch)  78.7 us
    unnamed x630, local copies, waits for them, and re-layouts  72.2 us
    slice x24, local copies, waits for them, and re-layouts, reduce_solve(): lower_even = lower_pair[:, 0]  61.6 us
  transfers between devices with their start and end apart: 1, of which 1 were waited for; matrix products, arithmetic and copies ran while one was open for 2% of the time, Pallas kernels for 0%

commit v1 on v0

v1 whole, which is shorter than its diff:
```python
import functools

import jax
import jax.numpy as jnp
from jax import lax
from jax.experimental import pallas as pl
from jax.experimental.pallas import tpu as pltpu
from jax.sharding import PartitionSpec as P

ITERS = 2
LANES = 128
SUB = 8
PARTS = 5
Y_BLOCKS = 16


def row_slice(tiles, i):
    return pl.ds((i // SUB) * (tiles * SUB) + i % SUB, tiles, stride=SUB)


def eliminate(w, r, q, d):
    s = w + q
    m = 1.0 / (1.0 + s)
    return m, s * m, m * (r + d)


def summarise(steps, unroll, blocks, shape, fetch, keep=None):
    zero = jnp.zeros(shape, jnp.float32)
    one = jnp.ones(shape, jnp.float32)

    def body(g, carry):
        for u in range(unroll):
            step = g * unroll + u
            new = []
            for b in range(blocks):
                total_g, d, total_s, prod, m, q = carry[b]
                w, r = fetch(b, step)
                m, q, d = eliminate(w, r, q, d)
                if keep is not None:
                    keep(b, step, m)
                after = prod * m
                new.append((total_g + prod * d, d, total_s + prod * after, after, m, q))
            carry = tuple(new)
        return carry

    start = tuple((zero, zero, zero, one, zero, one) for _ in range(blocks))
    done = lax.fori_loop(0, steps // unroll, body, start)
    return [block[:PARTS] for block in done]


def merge(a, b):
    ga, da, sa, pa, ma = a
    gb, db, sb, pb, mb = b
    den = 1.0 / (1.0 - ma * sb)
    return (
        ga + pa * ((gb + sb * da) * den),
        db + pb * ((da + ma * gb) * den),
        sa + pa * pa * sb * den,
        pa * pb * den,
        mb + pb * pb * ma * den,
    )


def x_summary(rows, tiles, fetch, loc_ref, sum_ref):
    half = rows // 2
    blocks = summarise(half, 2, 2, (tiles, LANES), lambda b, step: fetch(b * half + step))
    for b in range(2):
        for part in range(PARTS):
            loc_ref[pl.ds((b * PARTS + part) * tiles, tiles), :] = blocks[b][part]
    merged = merge(blocks[0], blocks[1])
    for part in range(PARTS):
        sum_ref[pl.ds(part * tiles, tiles), :] = merged[part]


def first_kernel(rows, tiles, v_ref, w_ref, rhs_ref, loc_ref, sum_ref):
    shape = (tiles, LANES)
    lane = lax.broadcasted_iota(jnp.int32, shape, 1)
    tile = lax.broadcasted_iota(jnp.int32, shape, 0)

    def fetch(i):
        at = row_slice(tiles, i)
        v = v_ref[at, :]
        w = w_ref[at, :]
        turned = pltpu.roll(v, 1, 1)
        left = jnp.where(lane == 0, jnp.where(tile == 0, 0.0, pltpu.roll(turned, 1, 0)), turned)
        turned = pltpu.roll(v, LANES - 1, 1)
        right = jnp.where(
            lane == LANES - 1,
            jnp.where(tile == tiles - 1, 0.0, pltpu.roll(turned, tiles - 1, 0)),
            turned,
        )
        r = w * v + ((left - v) + (right - v))
        rhs_ref[at, :] = r
        return w, r

    x_summary(rows, tiles, fetch, loc_ref, sum_ref)


def outer_kernel(axes, sizes, all_ref, out_ref):
    me = lax.axis_index(axes[0]) * sizes[1] + lax.axis_index(axes[1])
    count = sizes[0] * sizes[1]

    def part(p, k):
        return all_ref[p, k]

    zero = jnp.zeros(all_ref.shape[2:], jnp.float32)

    def prefix(p, carry):
        dd, mm = carry
        g, d, s, pp, m = (part(p, k) for k in range(PARTS))
        den = 1.0 / (1.0 - mm * s)
        return d + pp * ((dd + mm * g) * den), m + pp * pp * mm * den

    def suffix(step, carry):
        gg, ss = carry
        p = count - 1 - step
        g, d, s, pp, m = (part(p, k) for k in range(PARTS))
        den = 1.0 / (1.0 - m * ss)
        return g + pp * ((gg + ss * d) * den), s + pp * pp * ss * den

    dd, mm = lax.fori_loop(0, me, prefix, (zero, zero))
    gg, ss = lax.fori_loop(0, count - 1 - me, suffix, (zero, zero))
    g, d, s, pp, m = (part(me, k) for k in range(PARTS))
    a11 = 1.0 - mm * s
    a22 = 1.0 - ss * m
    a12 = mm * pp
    a21 = ss * pp
    b1 = dd + mm * g
    b2 = gg + ss * d
    det = 1.0 / (a11 * a22 - a12 * a21)
    out_ref[0] = (a22 * b1 + a12 * b2) * det
    out_ref[1] = (a11 * b2 + a21 * b1) * det


def step_kernel(
    rows, tiles, last,
    w_ref, rhs_ref, loc_ref, outer_ref, out_ref, *rest,
):
    if last:
        m_ref, d_ref, wt_ref, rt_ref, small_ref = rest
    else:
        loc_out, sum_out, m_ref, d_ref, wt_ref, rt_ref, small_ref = rest
    half = rows // 2

    xl = outer_ref[0]
    xr = outer_ref[1]
    (ga, da, sa, pa, ma), (gb, db, sb, pb, mb) = [
        [loc_ref[pl.ds((b * PARTS + k) * tiles, tiles), :] for k in range(PARTS)] for b in range(2)
    ]
    den = 1.0 / (1.0 - ma * sb)
    first_b = (gb + pb * xr + sb * (da + pa * xl)) * den
    last_a = da + pa * xl + ma * first_b

    unroll = 2

    def x_forward(g, carry):
        for u in range(unroll):
            step = g * unroll + u
            new = []
            for b in range(2):
                q, d = carry[b]
                i = b * half + step
                at = row_slice(tiles, i)
                m, q, d = eliminate(w_ref[at, :], rhs_ref[at, :], q, d)
                to = pl.ds(i * tiles, tiles)
                m_ref[to, :] = m
                d_ref[to, :] = d
                new.append((q, d))
            carry = tuple(new)
        return carry

    one = jnp.ones((tiles, LANES), jnp.float32)
    lax.fori_loop(0, half // unroll, x_forward, ((one, xl), (one, last_a)))

    def x_backward(g, carry):
        for u in range(unroll):
            step = half - 1 - (g * unroll + u)
            new = []
            for b in range(2):
                i = b * half + step
                to = pl.ds(i * tiles, tiles)
                at = row_slice(tiles, i)
                x = d_ref[to, :] + m_ref[to, :] * carry[b]
                out_ref[at, :] = 2.0 * w_ref[at, :] * x - rhs_ref[at, :]
                new.append(x)
            carry = tuple(new)
        return carry

    lax.fori_loop(0, half // unroll, x_backward, (first_b, xr))

    row_tiles = rows // LANES
    kblocks = Y_BLOCKS
    length = tiles * LANES // kblocks
    region = length * row_tiles + SUB
    groups = LANES // SUB

    def natural(rt, t, k):
        return pl.ds(pl.multiple_of(((rt * groups + k) * tiles + t) * SUB, SUB), SUB)

    def turned_at(rt, t, k):
        j = t * LANES
        block = j // length
        s = j % length
        return pl.ds(
            pl.multiple_of(block * region + ((s // SUB + k) * row_tiles + rt) * SUB, SUB), SUB
        )

    def turn(source, target, from_at, to_at, rt, t):
        block = jnp.concatenate([source[from_at(rt, t, k), :] for k in range(groups)], axis=0)
        block = block.T
        for k in range(groups):
            target[to_at(rt, t, k), :] = block[k * SUB:(k + 1) * SUB, :]

    def turn_there(g, carry):
        rt = g // tiles
        t = g % tiles
        turn(out_ref, rt_ref, natural, turned_at, rt, t)
        turn(w_ref, wt_ref, natural, turned_at, rt, t)
        return carry

    lax.fori_loop(0, row_tiles * tiles, turn_there, 0)

    width = row_tiles * kblocks

    def y_slices(step):
        base = (step // SUB) * (row_tiles * SUB) + step % SUB
        return [pl.ds(base + rt * SUB, kblocks, stride=region) for rt in range(row_tiles)]

    def y_load(ref, step):
        return jnp.concatenate([ref[at, :] for at in y_slices(step)], axis=0)

    def y_keep(b, step, m):
        m_ref[pl.ds(step * width, width), :] = m

    (parts,) = summarise(
        length, 2, 1, (width, LANES), lambda b, step: (y_load(wt_ref, step), y_load(rt_ref, step)), y_keep
    )
    for k in range(PARTS):
        small_ref[pl.ds(k * width, width), :] = parts[k]

    def y_part(k, block):
        return small_ref[pl.ds(k * width + block, row_tiles, stride=kblocks), :]

    nothing = jnp.zeros((row_tiles, LANES), jnp.float32)
    before = [(nothing, nothing)]
    for block in range(kblocks - 1):
        dd, mm = before[-1]
        g, d, s, pp, m = (y_part(k, block) for k in range(PARTS))
        den = 1.0 / (1.0 - mm * s)
        before.append((d + pp * ((dd + mm * g) * den), m + pp * pp * mm * den))
    after = nothing
    for block in reversed(range(kblocks)):
        dd, mm = before[block]
        g = y_part(0, block)
        s = y_part(2, block)
        pp = y_part(3, block)
        head = (g + s * dd + pp * after) / (1.0 - s * mm)
        small_ref[pl.ds(PARTS * width + block, row_tiles, stride=kblocks), :] = dd + mm * head
        small_ref[pl.ds((PARTS + 1) * width + block, row_tiles, stride=kblocks), :] = after
        after = head

    y_unroll = 4

    def y_forward(g, d):
        for u in range(y_unroll):
            step = g * y_unroll + u
            to = pl.ds(step * width, width)
            d = m_ref[to, :] * (y_load(rt_ref, step) + d)
            d_ref[to, :] = d
        return d

    lax.fori_loop(0, length // y_unroll, y_forward, small_ref[pl.ds(PARTS * width, width), :])

    def y_backward(g, x):
        for u in range(y_unroll):
            step = length - 1 - (g * y_unroll + u)
            to = pl.ds(step * width, width)
            x = d_ref[to, :] + m_ref[to, :] * x
            for rt, at in enumerate(y_slices(step)):
                piece = x[rt * kblocks:(rt + 1) * kblocks, :]
                if last:
                    rt_ref[at, :] = piece
                else:
                    rt_ref[at, :] = 2.0 * wt_ref[at, :] * piece - rt_ref[at, :]
        return x

    lax.fori_loop(0, length // y_unroll, y_backward, small_ref[pl.ds((PARTS + 1) * width, width), :])

    def turn_back(g, carry):
        rt = 2 * (g // tiles)
        t = g % tiles
        for more in range(2 if row_tiles % 2 == 0 else 1):
            turn(rt_ref, out_ref, turned_at, natural, rt + more, t)
        return carry

    if row_tiles % 2 == 0:
        lax.fori_loop(0, row_tiles * tiles // 2, turn_back, 0)
    else:
        def turn_single(g, carry):
            turn(rt_ref, out_ref, turned_at, natural, g // tiles, g % tiles)
            return carry

        lax.fori_loop(0, row_tiles * tiles, turn_single, 0)

    if not last:
        def fetch(i):
            at = row_slice(tiles, i)
            return w_ref[at, :], out_ref[at, :]

        x_summary(rows, tiles, fetch, loc_out, sum_out)


def solution(mesh):
    axes = tuple(mesh.axis_names)
    sizes = tuple(mesh.shape[a] for a in axes)
    vmem = pl.BlockSpec(memory_space=pltpu.VMEM)
    params = pltpu.CompilerParams(vmem_limit_bytes=66 * 1000 * 1000)

    def local(initial_field, diffusion):
        rows, columns = initial_field.shape
        tiles = columns // LANES
        cells = rows * tiles

        def flat(values):
            values = values.reshape(rows // SUB, SUB, tiles, LANES)
            return values.transpose(0, 2, 1, 3).reshape(cells, LANES)

        def unflat(values):
            values = values.reshape(rows // SUB, tiles, SUB, LANES)
            return values.transpose(0, 2, 1, 3).reshape(rows, columns)

        def shape(count):
            return jax.ShapeDtypeStruct((count, LANES), jnp.float32)

        field = shape(cells)
        loc = shape(2 * PARTS * tiles)
        summary = shape(PARTS * tiles)
        w = 2.0 / flat(diffusion).astype(jnp.float32)
        rhs, local_summary, own = pl.pallas_call(
            functools.partial(first_kernel, rows, tiles),
            out_shape=(field, loc, summary),
            in_specs=[vmem] * 2,
            out_specs=[vmem] * 3,
            compiler_params=params,
            name="first",
        )(flat(initial_field), w)
        turned = cells + Y_BLOCKS * SUB
        width = rows // LANES * Y_BLOCKS
        for iteration in range(ITERS):
            last = iteration == ITERS - 1
            everyone = lax.all_gather(own, axes, axis=0, tiled=True)
            count = sizes[0] * sizes[1]
            chunk = min(tiles, 32)
            outer = pl.pallas_call(
                functools.partial(outer_kernel, axes, sizes),
                grid=(tiles // chunk,),
                out_shape=jax.ShapeDtypeStruct((2, tiles, LANES), jnp.float32),
                in_specs=[pl.BlockSpec((count, PARTS, chunk, LANES), lambda c: (0, 0, c, 0))],
                out_specs=pl.BlockSpec((2, chunk, LANES), lambda c: (0, c, 0)),
                name="outer",
            )(everyone.reshape(count, PARTS, tiles, LANES))
            result = pl.pallas_call(
                functools.partial(step_kernel, rows, tiles, last),
                out_shape=(field,) if last else (field, loc, summary),
                in_specs=[vmem] * 4,
                out_specs=[vmem] * (1 if last else 3),
                scratch_shapes=[
                    pltpu.VMEM((cells, LANES), jnp.float32),
                    pltpu.VMEM((cells, LANES), jnp.float32),
                    pltpu.VMEM((turned, LANES), jnp.float32),
                    pltpu.VMEM((turned, LANES), jnp.float32),
                    pltpu.VMEM(((PARTS + 2) * width, LANES), jnp.float32),
                ],
                compiler_params=params,
                name="last" if last else "middle",
            )(w, rhs, local_summary, outer)
            if last:
                return unflat(result[0])
            rhs, local_summary, own = result

    in_specs = (P(axes, None), P(axes, None))
    return jax.shard_map(local, mesh=mesh, in_specs=in_specs, out_specs=P(axes, None), check_vma=False)
```

time: 1870 us -> 292 us (0.16)
  local copies, waits for them, and re-layouts: 794 us -> 0 us
  blocking collectives: 751 us -> 0 us
  other arithmetic: 242 us -> 6.59 us
  Pallas kernels: 0 us -> 154 us
  waiting for transfers between devices: 60.1 us -> 117 us
    all_to_all x4 -> x0, blocking collectives: 751 us -> none  [the longest x2 376 us: toward_x_lines(): lax.all_to_all(across_first, ('rows', 'cols'), split_axis=1, concat_axis=...]
    slice x193 -> x0, local copies, waits for them, and re-layouts: 333 us -> none  [the longest x95 117 us: lift_lines(): return jnp.concatenate([values[1:], jnp.zeros_like(values[:1])], axis=0)]
    another operation x68 -> x0, local copies, waits for them, and re-layouts: 165 us -> none  [reduce_solve(): return jnp.stack([even_values, coarse], axis=1).reshape(length, batch)]
    reshape x65 -> x0, local copies, waits for them, and re-layouts: 161 us -> none  [the longest x22 56.3 us: reduce_solve(): right_pair = right_side.reshape(halved, 2, batch)]
    pallas_call x0 -> x5, Pallas kernels: none -> 154 us  [the longest x2 124 us: local(): pl.pallas_call(functools.partial(step_kernel, rows, tiles, last), out_sha...]
    all_gather x0 -> x2, waiting for transfers between devices: none -> 117 us  [local(): everyone = lax.all_gather(own, axes, axis=0, tiled=True)]
    div x68 -> x1, other arithmetic: 103 us -> 6.59 us  [local(): w = 2.0 / flat(diffusion).astype(jnp.float32)]
    another operation x100 -> x0, other arithmetic: 78.7 us -> none  [reduce_solve(): return jnp.stack([even_values, coarse], axis=1).reshape(length, batch)]
  transfers between devices with their start and end apart: 1 -> 2, of which waited for: 1 -> 2; matrix products, arithmetic and copies ran while one was open for 2% -> 0% of each run, Pallas kernels for 0% -> 0%
where the time goes in v1:
time: 292 us
  Pallas kernels  154 us (53%)
  waiting for transfers between devices  117 us (40%)
  between operations  13.4 us (5%)
  other arithmetic  6.59 us (2%)
    pallas_call x2, Pallas kernels, local(): pl.pallas_call(functools.partial(step_kernel, rows, tiles, last), out_sha...  124 us
    all_gather x2, waiting for transfers between devices, local(): everyone = lax.all_gather(own, axes, axis=0, tiled=True)  117 us
    pallas_call x1, Pallas kernels, local(): pl.pallas_call(functools.partial(first_kernel, rows, tiles), out_shape=(f...  25 us
    div x1, other arithmetic, local(): w = 2.0 / flat(diffusion).astype(jnp.float32)  6.59 us
  transfers between devices with their start and end apart: 2, of which 2 were waited for; matrix products, arithmetic and copies ran while one was open for 0% of the time, Pallas kernels for 0%

profile of v1, /device:TPU:0, one launch (start us, length us, event | category | flops | bytes accessed | tf_op | source)
XLA Modules:
  0.0 291.7 jit_solution(5947519913600349857)
XLA Ops:
  6.5 0.0 all-gather.3.cloned.1.call-start
  6.5 6.6 %convert_divide_fusion = f32[512,4096]{1,0:T(8,128)} fusion(bf16[512,4096]{1,0:T(8,128)(2,1)} %param.3), kind=kLoop, calls=%fused_computation | loop fusion | flops 4194304 | bytes 12582912 | tf_op jit(solution)/shard_map/div | solution.py:338
  13.1 25.0 %first.1 = (f32[16384,128]{1,0:T(8,128)}, f32[320,128]{1,0:T(8,128)}, f32[160,128]{1,0:T(8,128)}) custom-call(f32[16384,128]{1,0:T(8,128)} %bitcast.20, f32[16384,128]{1,0:T(8,128)} %bitcast.17), custom_call_target="tpu_custom_call" | custom-call | tf_op jit(solution)/shard_map/first/pallas_call | solution.py:339
  38.2 0.0 all-gather.3.cloned.1.call-update
  38.2 0.0 all-gather.5.cloned.1.call-start
  38.2 60.6 %all-gather.3.cloned.1.call-done = f32[5120,128]{1,0:T(8,128)} async-done(((f32[160,128]{1,0:T(8,128)}), f32[5120,128]{1,0:T(8,128)}) %all-gather.3.cloned.1.call-update) | async-done | bytes 2621456 | tf_op jit(solution)/shard_map/all_gather | solution.py:351
  98.8 2.8 outer.2.outer_ref
  101.6 66.8 %middle.1 = (f32[16384,128]{1,0:T(8,128)}, f32[320,128]{1,0:T(8,128)}, f32[160,128]{1,0:T(8,128)}) custom-call(f32[16384,128]{1,0:T(8,128)} %bitcast.18, f32[16384,128]{1,0:T(8,128)} %get-tuple-element.11.rhs_ref, f32[320,128]{1,0:T(8,128)} %get-tuple-element.12.loc_ref, f32[2,32,128]{2,1,0:T(8,128)} %outer.2.outer_ref), custom_call_target="tpu_custom_call" | custom-call | tf_op jit(solution)/shard_map/middle/pallas_call | solution.py:362
  168.5 0.0 all-gather.5.cloned.1.call-update
  168.5 56.7 %all-gather.5.cloned.1.call-done = f32[5120,128]{1,0:T(8,128)} async-done(((f32[160,128]{1,0:T(8,128)}), f32[5120,128]{1,0:T(8,128)}) %all-gather.5.cloned.1.call-update) | async-done | bytes 2621456 | tf_op jit(solution)/shard_map/all_gather | solution.py:351
  225.2 2.8 outer.3.outer_ref
  228.0 56.8 %last.1 = f32[16384,128]{1,0:T(8,128)} custom-call(f32[16384,128]{1,0:T(8,128)} %bitcast.19, f32[16384,128]{1,0:T(8,128)} %get-tuple-element.14.rhs_ref, f32[320,128]{1,0:T(8,128)} %get-tuple-element.15.loc_ref, f32[2,32,128]{2,1,0:T(8,128)} %outer.3.outer_ref), custom_call_target="tpu_custom_call" | custom-call | tf_op jit(solution)/shard_map/last/pallas_call | solution.py:362
Async XLA Ops:
  6.5 92.3 %all-gather.3.cloned.1.call-start = ((), (), s32[]{:S(2)}) async-start(), calls=%async_computation | async-start | bytes 2703360 | tf_op jit(solution)/shard_map/all_gather | solution.py:351
  38.2 187.0 %all-gather.5.cloned.1.call-start = ((), (), s32[]{:S(2)}) async-start(), calls=%async_computation.1 | async-start | bytes 2703360 | tf_op jit(solution)/shard_map/all_gather | solution.py:351
Sparse Core Ops, SparseCore 0:
  38.3 60.4 all-gather.2
  168.6 56.5 all-gather.4

commit v2 on v1

--- a/solution.py
+++ b/solution.py
@@ -96,40 +96,29 @@
     x_summary(rows, tiles, fetch, loc_ref, sum_ref)
 
 
-def outer_kernel(axes, sizes, all_ref, out_ref):
-    me = lax.axis_index(axes[0]) * sizes[1] + lax.axis_index(axes[1])
-    count = sizes[0] * sizes[1]
-
-    def part(p, k):
-        return all_ref[p, k]
-
+def outer_kernel(count, all_ref, out_ref, keep_ref):
     zero = jnp.zeros(all_ref.shape[2:], jnp.float32)
 
     def prefix(p, carry):
         dd, mm = carry
-        g, d, s, pp, m = (part(p, k) for k in range(PARTS))
+        out_ref[p, 0] = dd
+        keep_ref[p] = mm
+        g, d, s, pp, m = (all_ref[p, k] for k in range(PARTS))
         den = 1.0 / (1.0 - mm * s)
         return d + pp * ((dd + mm * g) * den), m + pp * pp * mm * den
 
-    def suffix(step, carry):
-        gg, ss = carry
+    def suffix(step, after):
         p = count - 1 - step
-        g, d, s, pp, m = (part(p, k) for k in range(PARTS))
-        den = 1.0 / (1.0 - m * ss)
-        return g + pp * ((gg + ss * d) * den), s + pp * pp * ss * den
-
-    dd, mm = lax.fori_loop(0, me, prefix, (zero, zero))
-    gg, ss = lax.fori_loop(0, count - 1 - me, suffix, (zero, zero))
-    g, d, s, pp, m = (part(me, k) for k in range(PARTS))
-    a11 = 1.0 - mm * s
-    a22 = 1.0 - ss * m
-    a12 = mm * pp
-    a21 = ss * pp
-    b1 = dd + mm * g
-    b2 = gg + ss * d
-    det = 1.0 / (a11 * a22 - a12 * a21)
-    out_ref[0] = (a22 * b1 + a12 * b2) * det
-    out_ref[1] = (a11 * b2 + a21 * b1) * det
+        dd = out_ref[p, 0]
+        mm = keep_ref[p]
+        s = all_ref[p, 2]
+        head = (all_ref[p, 0] + s * dd + all_ref[p, 3] * after) / (1.0 - s * mm)
+        out_ref[p, 0] = dd + mm * head
+        out_ref[p, 1] = after
+        return head
+
+    lax.fori_loop(0, count, prefix, (zero, zero))
+    lax.fori_loop(0, count, suffix, zero)
 
 
 def step_kernel(
@@ -348,17 +337,20 @@
         width = rows // LANES * Y_BLOCKS
         for iteration in range(ITERS):
             last = iteration == ITERS - 1
-            everyone = lax.all_gather(own, axes, axis=0, tiled=True)
             count = sizes[0] * sizes[1]
-            chunk = min(tiles, 32)
-            outer = pl.pallas_call(
-                functools.partial(outer_kernel, axes, sizes),
-                grid=(tiles // chunk,),
-                out_shape=jax.ShapeDtypeStruct((2, tiles, LANES), jnp.float32),
-                in_specs=[pl.BlockSpec((count, PARTS, chunk, LANES), lambda c: (0, 0, c, 0))],
-                out_specs=pl.BlockSpec((2, chunk, LANES), lambda c: (0, c, 0)),
+            share = tiles // count
+            mine = own.reshape(PARTS, count, share, LANES).transpose(1, 0, 2, 3)
+            everyone = lax.all_to_all(mine, axes, split_axis=0, concat_axis=0, tiled=True)
+            solved = pl.pallas_call(
+                functools.partial(outer_kernel, count),
+                out_shape=jax.ShapeDtypeStruct((count, 2, share, LANES), jnp.float32),
+                in_specs=[vmem],
+                out_specs=vmem,
+                scratch_shapes=[pltpu.VMEM((count, share, LANES), jnp.float32)],
                 name="outer",
-            )(everyone.reshape(count, PARTS, tiles, LANES))
+            )(everyone)
+            outer = lax.all_to_all(solved, axes, split_axis=0, concat_axis=0, tiled=True)
+            outer = outer.transpose(1, 0, 2, 3).reshape(2, tiles, LANES)
             result = pl.pallas_call(
                 functools.partial(step_kernel, rows, tiles, last),
                 out_shape=(field,) if last else (field, loc, summary),

time: 292 us -> 208 us (0.71)
  waiting for transfers between devices: 117 us -> 0 us
  blocking collectives: 0 us -> 45.1 us
  between operations: 13.4 us -> 0.01 us
  local copies, waits for them, and re-layouts: 0 us -> 3.16 us
    all_gather x2 -> x0, waiting for transfers between devices: 117 us -> none  [local(): everyone = lax.all_gather(own, axes, axis=0, tiled=True)]
    all_to_all x0 -> x4, blocking collectives: none -> 45.1 us  [the longest x2 25.3 us: local(): lax.all_to_all(mine, axes, split_axis=0, concat_axis=0, tiled=True)]
  transfers between devices with their start and end apart: 2 -> 0, of which waited for: 2 -> 0; matrix products, arithmetic and copies ran while one was open for 0% -> 0% of each run, Pallas kernels for 0% -> 0%
where the time goes in v2:
time: 208 us
  Pallas kernels  153 us (74%)
  blocking collectives  45.1 us (22%)
  other arithmetic  6.56 us (3%)
  local copies, waits for them, and re-layouts  3.16 us (2%)
    pallas_call x2, Pallas kernels, local(): pl.pallas_call(functools.partial(step_kernel, rows, tiles, last), out_sha...  124 us
    all_to_all x2, blocking collectives, local(): lax.all_to_all(mine, axes, split_axis=0, concat_axis=0, tiled=True)  25.3 us
    pallas_call x1, Pallas kernels, local(): pl.pallas_call(functools.partial(first_kernel, rows, tiles), out_shape=(f...  25 us
    all_to_all x2, blocking collectives, local(): lax.all_to_all(solved, axes, split_axis=0, concat_axis=0, tiled=True)  19.8 us
    div x1, other arithmetic, local(): w = 2.0 / flat(diffusion).astype(jnp.float32)  6.56 us
    pallas_call x2, Pallas kernels, local(): pl.pallas_call(functools.partial(outer_kernel, count), out_shape=jax.Shap...  4.59 us

profile of v2, /device:TPU:0, one launch (start us, length us, event | category | flops | bytes accessed | tf_op | source)
XLA Modules:
  0.0 208.1 jit_solution(3410188575363114403)
XLA Ops:
  0.0 6.6 %convert_divide_fusion = f32[512,4096]{1,0:T(8,128)} fusion(bf16[512,4096]{1,0:T(8,128)(2,1)} %param.3), kind=kLoop, calls=%fused_computation | loop fusion | flops 4194304 | bytes 12582912 | tf_op jit(solution)/shard_map/div | solution.py:327
  6.6 25.0 %first.1 = (f32[16384,128]{1,0:T(8,128)}, f32[320,128]{1,0:T(8,128)}, f32[160,128]{1,0:T(8,128)}) custom-call(f32[16384,128]{1,0:T(8,128)} %bitcast.38, f32[16384,128]{1,0:T(8,128)} %bitcast.35), custom_call_target="tpu_custom_call" | custom-call | tf_op jit(solution)/shard_map/first/pallas_call | solution.py:328
  31.6 1.0 copy.20
  32.6 15.1 %all_to_all.20.all_ref = f32[32,5,1,128]{3,2,1,0:T(1,128)} all-to-all(f32[32,5,1,128]{3,2,1,0:T(1,128)S(1)} %bitcast.39), channel_id=1, replica_groups=mesh['rows'=16,'cols'=2] {'rows','cols'}, dimensions={0} | all-to-all | bytes 163840 | tf_op jit(solution)/shard_map/all_to_all | solution.py:343
  47.6 2.3 %outer.2 = f32[32,2,1,128]{3,2,1,0:T(1,128)} custom-call(f32[32,5,1,128]{3,2,1,0:T(1,128)} %all_to_all.20.all_ref), custom_call_target="tpu_custom_call" | custom-call | tf_op jit(solution)/shard_map/outer/pallas_call | solution.py:344
  49.9 9.9 %all_to_all.21 = f32[32,2,1,128]{3,1,2,0:T(2,128)S(1)} all-to-all(f32[32,2,1,128]{3,1,2,0:T(2,128)} %bitcast.43), channel_id=1, replica_groups=mesh['rows'=16,'cols'=2] {'rows','cols'}, dimensions={0} | all-to-all | bytes 65536 | tf_op jit(solution)/shard_map/all_to_all | solution.py:352
  59.8 0.6 copy.22
  60.4 66.8 %middle.1 = (f32[16384,128]{1,0:T(8,128)}, f32[320,128]{1,0:T(8,128)}, f32[160,128]{1,0:T(8,128)}) custom-call(f32[16384,128]{1,0:T(8,128)} %bitcast.36, f32[16384,128]{1,0:T(8,128)} %get-tuple-element.11.rhs_ref, f32[320,128]{1,0:T(8,128)} %get-tuple-element.12.loc_ref, f32[2,32,128]{2,1,0:T(8,128)} %bitcast.41), custom_call_target="tpu_custom_call" | custom-call | tf_op jit(solution)/shard_map/middle/pallas_call | solution.py:354
  127.2 1.0 copy.19
  128.2 10.2 %all_to_all.22.all_ref = f32[32,5,1,128]{3,2,1,0:T(1,128)} all-to-all(f32[32,5,1,128]{3,2,1,0:T(1,128)S(1)} %bitcast.40), channel_id=1, replica_groups=mesh['rows'=16,'cols'=2] {'rows','cols'}, dimensions={0} | all-to-all | bytes 163840 | tf_op jit(solution)/shard_map/all_to_all | solution.py:343
  138.4 2.3 %outer.3 = f32[32,2,1,128]{3,2,1,0:T(1,128)} custom-call(f32[32,5,1,128]{3,2,1,0:T(1,128)} %all_to_all.22.all_ref), custom_call_target="tpu_custom_call" | custom-call | tf_op jit(solution)/shard_map/outer/pallas_call | solution.py:344
  140.7 9.9 %all_to_all.23 = f32[32,2,1,128]{3,1,2,0:T(2,128)S(1)} all-to-all(f32[32,2,1,128]{3,1,2,0:T(2,128)} %bitcast.44), channel_id=1, replica_groups=mesh['rows'=16,'cols'=2] {'rows','cols'}, dimensions={0} | all-to-all | bytes 65536 | tf_op jit(solution)/shard_map/all_to_all | solution.py:352
  150.6 0.6 copy.21
  151.2 56.8 %last.1 = f32[16384,128]{1,0:T(8,128)} custom-call(f32[16384,128]{1,0:T(8,128)} %bitcast.37, f32[16384,128]{1,0:T(8,128)} %get-tuple-element.14.rhs_ref, f32[320,128]{1,0:T(8,128)} %get-tuple-element.15.loc_ref, f32[2,32,128]{2,1,0:T(8,128)} %bitcast.42), custom_call_target="tpu_custom_call" | custom-call | tf_op jit(solution)/shard_map/last/pallas_call | solution.py:354
